TPU v7x, 128 devices: a 2x2x16 block of a 8x8x16 slice. The times are simulated.
128 devices in a mesh: groups: 4 (over x, y), lon: 16 (over z), lat: 2 (over core).
Axes of the slice: x: 2, y: 2, z: 16, core: 2. Of those that a mesh axis runs over, the one named last changes fastest.
The devices are a block of a 8x8x16 slice.
Arguments:
- fields: bfloat16 [48, 2048, 128], P(('groups', 'lat'), 'lon'), parts along dimension 0, may hold values from -6 to 6
- norm_gain: float32 [128], replicated, may hold values from 0.5 to 1.5
- w_qkv: bfloat16 [128, 384], replicated, may hold values from -5.303301 to 5.303301
- w_out: bfloat16 [128, 128], replicated, may hold values from -0.5 to 0.5
Outputs:
- updated: bfloat16 [48, 2048, 128], P(('groups', 'lat'), 'lon'), parts along dimension 0
There are 4 independent parts, one for each index of `groups`. A program takes and returns all parts, laid end to end along the dimension named above; an argument that names none is the same for every part. Nothing has to cross between parts.
All inputs are finite; a program needn't handle non-finite values.
Results may differ from a plain program's by a relative error of at most 0.005.
The roundings to bfloat16 on the way count: a program that leaves them out, or rounds other values in their place, can miss the bound.
Values may be sent and summed in bfloat16 or wider, within the bound.
A program may use at most 128 MiB of HBM per device.

v0:
```python
import math

import jax
import jax.numpy as jnp
from jax import lax
from jax.sharding import PartitionSpec as P

HEADS = 8


def attend_items(local):
    total_cells = local.shape[2]
    head_width = local.shape[3] // 3
    block = math.gcd(total_cells, 512)

    def one_item(item):
        item_keys = item[:, head_width : 2 * head_width]
        item_values = item[:, 2 * head_width :]
        query_blocks = item[:, :head_width].reshape(total_cells // block, block, head_width)

        def one_block(query_block):
            scores = jnp.dot(query_block, item_keys.T, preferred_element_type=jnp.float32)
            highest = jnp.max(scores, axis=-1, keepdims=True)
            expd = jnp.exp(scores - highest)
            totals = jnp.sum(expd, axis=-1, keepdims=True)
            mixed = jnp.dot(
                expd.astype(jnp.bfloat16), item_values, preferred_element_type=jnp.float32
            )
            return (mixed / totals).astype(jnp.bfloat16)

        return lax.map(one_block, query_blocks).reshape(total_cells, head_width)

    flat = local.reshape(local.shape[0] * local.shape[1], total_cells, 3 * head_width)
    results = lax.map(one_item, flat)
    return results.reshape(local.shape[0], local.shape[1], total_cells, head_width)


def body(fields, norm_gain, w_qkv, w_out):
    lat_rows, lon_cells, width = fields.shape
    head_count = HEADS
    head_width = width // head_count
    inputs = fields.astype(jnp.float32)
    center = jnp.mean(inputs, axis=-1, keepdims=True)
    spread = jnp.mean((inputs - center) ** 2, axis=-1, keepdims=True)
    normed = ((inputs - center) * lax.rsqrt(spread + 1e-05) * norm_gain).astype(jnp.bfloat16)
    projected = jnp.dot(normed.reshape(-1, width), w_qkv, preferred_element_type=jnp.float32)
    projected = projected.reshape(lat_rows, lon_cells, 3 * width)
    queries = (projected[..., :width] * (1.0 / math.sqrt(head_width))).astype(jnp.bfloat16)
    queries = queries.reshape(lat_rows, lon_cells, head_count, head_width)
    cycle_size = lax.axis_size("lon")
    key_part = (
        projected[..., width : 2 * width]
        .astype(jnp.bfloat16)
        .reshape(lat_rows, lon_cells, head_count, head_width)
    )
    value_part = (
        projected[..., 2 * width :]
        .astype(jnp.bfloat16)
        .reshape(lat_rows, lon_cells, head_count, head_width)
    )
    stacked = jnp.concatenate([queries, key_part, value_part], axis=-1)
    per_device = lat_rows * head_count // cycle_size
    stacked = jnp.transpose(stacked, (0, 2, 1, 3)).reshape(
        cycle_size, per_device, lon_cells, 3 * head_width
    )
    results = attend_items(lax.all_to_all(stacked, "lon", split_axis=0, concat_axis=2, tiled=True))
    returned = lax.all_to_all(results, "lon", split_axis=2, concat_axis=0, tiled=True)
    returned = returned.reshape(lat_rows, head_count, lon_cells, head_width)
    attended = jnp.transpose(returned, (0, 2, 1, 3)).reshape(lat_rows * lon_cells, width)
    output = jnp.dot(attended, w_out, preferred_element_type=jnp.float32)
    return (inputs + output.reshape(lat_rows, lon_cells, width)).astype(jnp.bfloat16)


def solution(mesh):
    return jax.shard_map(
        body,
        mesh=mesh,
        in_specs=(P(("groups", "lat"), "lon", None), P(), P(), P()),
        out_specs=P(("groups", "lat"), "lon", None),
        check_vma=False,
    )
```

profile of v0, /device:TPU:84, one launch (start us, length us, event | category | flops | bytes accessed | tf_op | source)
XLA Modules:
  0.0 115.5 jit_solution(17340997103180852078)
XLA Ops:
  0.0 0.0 copy-start
  0.0 1.1 convert_reduce_fusion
  1.1 1.2 %fusion.24 = f32[6,128]{1,0:T(8,128)S(1)} fusion(bf16[6,128,128]{2,1,0:T(8,128)(2,1)} %param.8, f32[6,128]{1,0:T(8,128)S(1)} %broadcast_multiply_fusion), kind=kLoop, calls=%fused_computation.23 | loop fusion | flops 392448 | bytes 202752 | tf_op jit(solution)/shard_map/reduce_sum | solution.py:44
  2.4 0.0 copy-done
  2.4 1.4 %fusion.38 = (bf16[6,128,384]{2,1,0:T(8,128)(2,1)S(1)}, f32[6,128,384]{2,1,0:T(8,128)S(1)}) fusion(bf16[128,384]{1,0:T(8,128)(2,1)S(1)} %copy-done, bf16[6,128,128]{2,1,0:T(8,128)(2,1)} %param.8, f32[128]{0:T(128)} %param.9, f32[6,128]{1,0:T(8,128)S(1)} %add_rsqrt_fusion, f32[6,128]{1,0:T(8,128)S(1)} %broadcast_multiply_fusion), kind=kOutput, calls=%fused_computation.39 | convolution fusion | flops 76283904 | bytes 2071040 | tf_op jit(solution)/shard_map/dot_general | solution.py:46
  3.7 0.1 fusion.37
  3.8 0.2 copy.23
  4.0 0.2 copy.24
  4.2 0.2 copy.22
  4.4 0.9 pad_maximum_fusion
  5.3 17.0 %all-to-all-start = ((bf16[16,3,128,48]{2,3,1,0:T(8,128)(2,1)}), bf16[16,3,128,48]{2,3,1,0:T(8,128)(2,1)S(1)}, u32[]{:S(2)}, u32[]{:S(2)}) async-start(bf16[16,3,128,48]{2,3,1,0:T(8,128)(2,1)} %bitcast.8), calls=%async_computation | async-start | bytes 1179648 | tf_op jit(solution)/shard_map/all_to_all | solution.py:66
  22.3 30.6 %all-to-all-done = bf16[16,3,128,48]{2,3,1,0:T(8,128)(2,1)S(1)} async-done(((bf16[16,3,128,48]{2,3,1,0:T(8,128)(2,1)}), bf16[16,3,128,48]{2,3,1,0:T(8,128)(2,1)S(1)}, u32[]{:S(2)}, u32[]{:S(2)}) %all-to-all-start) | async-done | bytes 589856 | tf_op jit(solution)/shard_map/all_to_all | solution.py:66
  52.9 0.2 copy.25
  53.1 0.3 reshape.55
  53.3 28.0 %while.21 = (s32[]{:T(128)}, bf16[3,2048,16]{1,2,0:T(8,128)(2,1)S(1)}, bf16[3,2048,48]{1,2,0:T(8,128)(2,1)S(1)}, s32[]{:T(128)}, s32[]{:T(128)}, /*index=5*/s32[]{:T(128)}) while((s32[]{:T(128)}, bf16[3,2048,16]{1,2,0:T(8,128)(2,1)S(1)}, bf16[3,2048,48]{1,2,0:T(8,128)(2,1)S(1)}, s32[]{:T(128)}, s32[]{:T(128)}, /*index=5*/s32[]{:T(128)}) %tuple.49), condition=%wide.region_7.8_spmd, body=%wide.region_2.7_spmd.sunk | while | flops 72367104 | bytes 14067922 | solution.py:34
  53.4 9.1 %while.22 = (s32[]{:T(128)}, bf16[4,512,16]{1,2,0:T(8,128)(2,1)S(1)}, bf16[4,512,16]{1,2,0:T(8,128)(2,1)S(1)}, bf16[2048,16]{0,1:T(8,128)(2,1)S(1)}, bf16[2048,16]{0,1:T(8,128)(2,1)S(1)}, /*index=5*/s32[]{:T(128)}) while((s32[]{:T(128)}, bf16[4,512,16]{1,2,0:T(8,128)(2,1)S(1)}, bf16[4,512,16]{1,2,0:T(8,128)(2,1)S(1)}, ...), condition=%wide.region_6.6_spmd, body=%wide.region_3.5_spmd.sunk | while | flops 72367104 | bytes 12757069 | solution.py:31
  53.4 0.8 fusion.53
  54.2 0.7 fusion.54
  55.0 0.8 fusion.55
  55.7 0.8 fusion.53
  56.5 0.7 fusion.54
  57.2 0.8 fusion.55
  58.0 0.8 fusion.53
  58.8 0.7 fusion.54
  59.5 0.8 fusion.55
  60.3 0.8 fusion.53
  61.1 0.7 fusion.54
  61.8 0.8 fusion.55
  62.6 0.1 copy.39
  62.8 9.1 %while.22 = (s32[]{:T(128)}, bf16[4,512,16]{1,2,0:T(8,128)(2,1)S(1)}, bf16[4,512,16]{1,2,0:T(8,128)(2,1)S(1)}, bf16[2048,16]{0,1:T(8,128)(2,1)S(1)}, bf16[2048,16]{0,1:T(8,128)(2,1)S(1)}, /*index=5*/s32[]{:T(128)}) while((s32[]{:T(128)}, bf16[4,512,16]{1,2,0:T(8,128)(2,1)S(1)}, bf16[4,512,16]{1,2,0:T(8,128)(2,1)S(1)}, ...), condition=%wide.region_6.6_spmd, body=%wide.region_3.5_spmd.sunk | while | flops 72367104 | bytes 12757069 | solution.py:31
  62.8 0.8 fusion.53
  63.6 0.7 fusion.54
  64.3 0.8 fusion.55
  65.1 0.8 fusion.53
  65.9 0.7 fusion.54
  66.6 0.8 fusion.55
  67.3 0.8 fusion.53
  68.2 0.7 fusion.54
  68.9 0.8 fusion.55
  69.6 0.8 fusion.53
  70.4 0.7 fusion.54
  71.2 0.8 fusion.55
  71.9 0.1 copy.39
  72.1 9.1 %while.22 = (s32[]{:T(128)}, bf16[4,512,16]{1,2,0:T(8,128)(2,1)S(1)}, bf16[4,512,16]{1,2,0:T(8,128)(2,1)S(1)}, bf16[2048,16]{0,1:T(8,128)(2,1)S(1)}, bf16[2048,16]{0,1:T(8,128)(2,1)S(1)}, /*index=5*/s32[]{:T(128)}) while((s32[]{:T(128)}, bf16[4,512,16]{1,2,0:T(8,128)(2,1)S(1)}, bf16[4,512,16]{1,2,0:T(8,128)(2,1)S(1)}, ...), condition=%wide.region_6.6_spmd, body=%wide.region_3.5_spmd.sunk | while | flops 72367104 | bytes 12757069 | solution.py:31
  72.1 0.8 fusion.53
  72.9 0.7 fusion.54
  73.7 0.8 fusion.55
  74.4 0.8 fusion.53
  75.2 0.7 fusion.54
  75.9 0.8 fusion.55
  76.7 0.8 fusion.53
  77.5 0.7 fusion.54
  78.2 0.8 fusion.55
  79.0 0.8 fusion.53
  79.8 0.7 fusion.54
  80.5 0.8 fusion.55
  81.3 0.1 copy.39
  81.4 1.4 %copy.26 = bf16[3,2048,16]{2,0,1:T(4,128)(2,1)S(1)} copy(bf16[3,2048,16]{1,2,0:T(8,128)(2,1)S(1)} %get-tuple-element.49) | data formatting | bytes 393216 | tf_op jit(solution)/shard_map/while | solution.py:34
  82.7 1.8 %bitcast_bitcast_fusion = bf16[2048,1,3,16]{3,2,1,0:T(4,128)(2,1)} fusion(bf16[3,2048,16]{2,0,1:T(4,128)(2,1)S(1)} %copy.26), kind=kLoop, calls=%fused_computation.40 | loop fusion | bytes 393216
  84.5 3.6 %reshape.60 = bf16[16,2,3072]{2,1,0:T(2,128)(2,1)S(1)} reshape(bf16[2048,1,3,16]{3,2,1,0:T(4,128)(2,1)} %bitcast_bitcast_fusion) | data formatting | bytes 393216
  88.1 23.7 %all_to_all.30 = bf16[16,2,3072]{2,1,0:T(2,128)(2,1)S(1)} all-to-all(bf16[16,2,3072]{2,1,0:T(2,128)(2,1)S(1)} %reshape.60), channel_id=1, replica_groups=mesh['groups'=4,'lon'=16,'lat'=2] {'lon'}, dimensions={0} | all-to-all | bytes 393216 | tf_op jit(solution)/shard_map/all_to_all | solution.py:67
  111.8 2.0 %reshape.61 = bf16[2048,1,3,16]{3,2,1,0:T(4,128)(2,1)S(1)} reshape(bf16[16,2,3072]{2,1,0:T(2,128)(2,1)S(1)} %all_to_all.30) | data formatting | bytes 393216
  113.8 0.8 copy.32
  114.6 0.9 fusion.21
  (26 shorter events, 0.3 us)
Async XLA Ops:
  0.0 2.4 %copy-start = (bf16[128,384]{1,0:T(8,128)(2,1)S(1)}, bf16[128,384]{1,0:T(8,128)(2,1)}, u32[]{:S(2)}) copy-start(bf16[128,384]{1,0:T(8,128)(2,1)} %param.10) | copy-start | bytes 294916
  5.3 47.7 %all-to-all-start = ((bf16[16,3,128,48]{2,3,1,0:T(8,128)(2,1)}), bf16[16,3,128,48]{2,3,1,0:T(8,128)(2,1)S(1)}, u32[]{:S(2)}, u32[]{:S(2)}) async-start(bf16[16,3,128,48]{2,3,1,0:T(8,128)(2,1)} %bitcast.8), calls=%async_computation | async-start | bytes 1179648 | tf_op jit(solution)/shard_map/all_to_all | solution.py:66
  111.8 2.8 %copy-start.1 = (bf16[6,128,128]{2,1,0:T(8,128)(2,1)S(1)}, bf16[6,128,128]{2,1,0:T(8,128)(2,1)}, u32[]{:S(2)}) copy-start(bf16[6,128,128]{2,1,0:T(8,128)(2,1)} %param.8) | copy-start | bytes 589828
  111.8 2.8 %copy-start.2 = (bf16[128,128]{1,0:T(8,128)(2,1)S(1)}, bf16[128,128]{1,0:T(8,128)(2,1)}, u32[]{:S(2)}) copy-start(bf16[128,128]{1,0:T(8,128)(2,1)} %param.11) | copy-start | bytes 98308
where the time goes:
time: 116 us
  waiting for transfers between devices  30.6 us (26%)
  blocking collectives  23.7 us (20%)
  matrix products  21.1 us (18%)
  starting transfers between devices  17 us (15%)
  other arithmetic  11.7 us (10%)
  local copies, waits for them, and re-layouts  10.9 us (9%)
    all_to_all x1, waiting for transfers between devices, body(): lax.all_to_all(stacked, 'lon', split_axis=0, concat_axis=2, tiled=True)  30.6 us
    all_to_all x1, blocking collectives, body(): lax.all_to_all(results, 'lon', split_axis=2, concat_axis=0, tiled=True)  23.7 us
    all_to_all x1, starting transfers between devices, body(): lax.all_to_all(stacked, 'lon', split_axis=0, concat_axis=2, tiled=True)  17 us
    dot_general x12, matrix products, one_block(): jnp.dot(query_block, item_keys.T, preferred_element_type=jnp.float32)  9.82 us
    dot_general x12, matrix products, one_block(): jnp.dot(expd.astype(jnp.bfloat16), item_values, preferred_element_type=jn...  9.03 us
    reduce_sum x12, other arithmetic, one_block(): totals = jnp.sum(expd, axis=-1, keepdims=True)  8.51 us
    unnamed x9, local copies, waits for them, and re-layouts  7.33 us
  transfers between devices with their start and end apart: 1, of which 1 were waited for; matrix products, arithmetic and copies ran while one was open for 0% of the time, Pallas kernels for 0%

commit v1 on v0

v1 whole, which is shorter than its diff:
```python
import functools
import math

import jax
import jax.numpy as jnp
from jax import lax
from jax.experimental import pallas as pl
from jax.experimental.pallas import tpu as pltpu
from jax.sharding import PartitionSpec as P

HEADS = 8
LOG2E = math.log2(math.e)
LOW = -1e30
F32 = jnp.float32
BF16 = jnp.bfloat16
MESH = pl.DeviceIdType.MESH


def kernel(
    n,
    fields_ref, gain_ref, wqkv_ref, wout_ref, out_ref,
    xin, gain, wqkv, wout, raw, nbuf, kd, vt, qt, qh, sbuf, mst, ost, alpha, att, obuf,
    load_sem, raw_send, raw_recv, fwd_send, out_send, out_recv, ready,
):
    rows, cells, width = xin.shape
    total_rows = 2 * rows
    half = cells // 2
    hw = width // HEADS
    span = 4 * cells
    keys = 8 * cells
    tiles = 4
    tile = keys // tiles

    p = lax.axis_index("lon")
    j = lax.axis_index("lat")
    right = {"lon": lax.rem(p + 1, n), "lat": j}
    left = {"lon": lax.rem(p + n - 1, n), "lat": j}
    partner = {"lon": p, "lat": 1 - j}

    loads = [
        pltpu.make_async_copy(fields_ref, xin, load_sem.at[0]),
        pltpu.make_async_copy(gain_ref, gain, load_sem.at[1]),
        pltpu.make_async_copy(wqkv_ref, wqkv, load_sem.at[2]),
        pltpu.make_async_copy(wout_ref, wout, load_sem.at[3]),
    ]
    for load in loads:
        load.start()

    barrier = pltpu.get_barrier_semaphore()
    for step in (1, n - 1):
        for core in (0, 1):
            pl.semaphore_signal(
                barrier, inc=1, device_id={"lon": lax.rem(p + step, n), "lat": core}, device_id_type=MESH
            )
    pl.semaphore_signal(barrier, inc=1, device_id=partner, device_id_type=MESH)

    def row_of(x):
        return (x * total_rows + n - 1) // n

    def takes_row(x):
        return (row_of(x) * n) // total_rows == x

    my_row = row_of(p)
    main = takes_row(p)
    my_lat = my_row // rows
    my_r = lax.rem(my_row, rows)

    def field_copy(d, h):
        x = lax.rem(p + n - d, n)
        r = lax.rem(row_of(x), rows)
        return pltpu.make_async_remote_copy(
            src_ref=xin.at[r, pl.ds(h * half, half)],
            dst_ref=raw.at[d, pl.ds(h * half, half)],
            send_sem=raw_send.at[d, h],
            recv_sem=raw_recv.at[d, h],
            device_id={"lon": x, "lat": h},
            device_id_type=MESH,
        )

    def own_field_copy(h):
        return pltpu.make_async_copy(
            fields_ref.at[my_r, pl.ds(h * half, half)], raw.at[0, pl.ds(h * half, half)], raw_recv.at[0, h]
        )

    def sends_to(d):
        x = lax.rem(p + n - d, n)
        return jnp.logical_and(takes_row(x), row_of(x) // rows == j)

    def start_fields(d):
        @pl.when(sends_to(d))
        def _():
            for h in (0, 1):
                if d == 0:
                    @pl.when(j == h)
                    def _():
                        own_field_copy(h).start()

                    @pl.when(j != h)
                    def _():
                        field_copy(d, h).start()
                else:
                    field_copy(d, h).start()

    def forward(d):
        return pltpu.make_async_remote_copy(
            src_ref=raw.at[d, pl.ds(j * half, half)],
            dst_ref=raw.at[d, pl.ds(j * half, half)],
            send_sem=fwd_send.at[d],
            recv_sem=raw_recv.at[d, j],
            device_id=partner,
            device_id_type=MESH,
        )

    def wait_half(d, h):
        pltpu.make_async_copy(
            fields_ref.at[0, pl.ds(0, half)], raw.at[d, pl.ds(h * half, half)], raw_recv.at[d, h]
        ).wait()

    def take(d):
        wait_half(d, j)
        forward(d).start()

    loads[0].wait()
    pl.semaphore_wait(barrier, 5)
    start_fields(0)
    for dist in range(1, n // 2 + 1):
        if dist > 1:
            for side in (right, left):
                pl.semaphore_signal(ready.at[dist - 2], inc=1, device_id=side, device_id_type=MESH)
            pl.semaphore_wait(ready.at[dist - 2], 2)
        start_fields(dist)
        if dist < n // 2:
            start_fields(n - dist)

    for load in loads[1:]:
        load.wait()

    def out_copy(g, k):
        d = own_chunk(g, k)
        return pltpu.make_async_remote_copy(
            src_ref=obuf.at[g, pl.ds(k * cells, cells)],
            dst_ref=out_ref.at[my_r],
            send_sem=out_send.at[g, k],
            recv_sem=out_recv.at[my_r],
            device_id={"lon": lax.rem(p + d, n), "lat": my_lat},
            device_id_type=MESH,
        )

    def own_out_copy():
        return pltpu.make_async_copy(obuf.at[0, pl.ds(0, cells)], out_ref.at[my_r], out_recv.at[my_r])

    def own_chunk(g, k):
        return 4 * g + k + j * (n - 1 - 8 * g - 2 * k)

    @pl.when(main)
    def _():
        wq = wqkv[:, :width]
        wk = wqkv[:, width : 2 * width]
        wv = wqkv[:, 2 * width :]
        for h in range(HEADS):
            vt[pl.ds(2 * hw * h + hw, hw), :] = jnp.ones((hw, n * cells), BF16)
        qh[...] = jnp.zeros_like(qh)
        mst[...] = jnp.full(mst.shape, LOW, F32)
        ost[...] = jnp.zeros_like(ost)

        def project(slot, d, place):
            x = raw[d].astype(F32)
            center = jnp.mean(x, axis=-1, keepdims=True)
            y = x - center
            spread = jnp.mean(y * y, axis=-1, keepdims=True)
            normed = (y * lax.rsqrt(spread + 1e-05) * gain[...]).astype(BF16)
            nbuf[place] = normed
            where = pl.ds(pl.multiple_of(slot * cells, cells), cells)
            k = jnp.dot(normed, wk, preferred_element_type=F32).astype(BF16)
            kd[where, :width] = k
            kd[where, width:] = k
            v = lax.dot_general(wv, normed, (((0,), (1,)), ((), ())), preferred_element_type=F32).astype(BF16)
            for h in range(HEADS):
                vt[2 * hw * h : 2 * hw * h + hw, where] = v[hw * h : hw * h + hw]

        def arrive(g):
            def first(k, carry):
                take(4 * g + k)
                take(n - 1 - 4 * g - k)
                return carry

            lax.fori_loop(0, 4, first, 0)

            def second(k, carry):
                for place in (0, 1):
                    d = 4 * g + k if place == 0 else n - 1 - 4 * g - k
                    wait_half(d, 1 - j)
                    project(8 * g + 4 * place + k, d, place)
                q = lax.dot_general(wq, nbuf[j], (((0,), (1,)), ((), ())), preferred_element_type=F32)
                q = (q * (1.0 / math.sqrt(hw))).astype(BF16).astype(F32) * LOG2E
                high = q.astype(BF16)
                low = (q - high.astype(F32)).astype(BF16)
                where = pl.ds(pl.multiple_of(k * cells, cells), cells)
                qt[g, :width, where] = high
                qt[g, width:, where] = low
                return carry

            lax.fori_loop(0, 4, second, 0)

        def scores(h, g, kb, slot):
            before = lax.rem(h + HEADS - 1, HEADS)
            for base in (0, width):
                qh[pl.ds(base + pl.multiple_of(before * hw, hw), hw), :] = jnp.zeros((hw, span), BF16)
            for base in (0, width):
                here = pl.ds(base + pl.multiple_of(h * hw, hw), hw)
                qh[here, :] = qt[g, here, :]
            high = None
            for t in range(tiles):
                s = jnp.dot(
                    kd[pl.ds(pl.multiple_of(kb * keys, keys) + t * tile, tile), :], qh[...], preferred_element_type=F32
                )
                sbuf[slot, pl.ds(t * tile, tile), :] = s
                top = jnp.max(s.reshape(tile // 8, 8, span), axis=0)
                high = top if high is None else jnp.maximum(high, top)
            old = mst[g, h]
            new = jnp.maximum(old, jnp.max(high, axis=0, keepdims=True))
            mst[g, h] = new
            alpha[slot, 0] = new
            alpha[slot, 1] = jnp.exp2(old - new)

        def values(h, g, kb, slot):
            top = alpha[slot, 0]
            total = ost[g, h] * alpha[slot, 1]
            for t in range(tiles):
                e = jnp.exp2(sbuf[slot, pl.ds(t * tile, tile), :] - top).astype(BF16)
                v = vt[
                    pl.ds(pl.multiple_of(2 * hw * h, 2 * hw), 2 * hw),
                    pl.ds(pl.multiple_of(kb * keys, keys) + t * tile, tile),
                ]
                total = total + jnp.dot(v, e, preferred_element_type=F32)
            ost[g, h] = total
            att[pl.ds(pl.multiple_of(h * hw, hw), hw), :] = (total[:hw] / total[hw:]).astype(BF16)

        def run(units):
            for g, kb in units:
                scores(0, g, kb, 0)

                def step(h, carry):
                    scores(h + 1, g, kb, lax.rem(h + 1, 2))
                    values(h, g, kb, lax.rem(h, 2))
                    return carry

                lax.fori_loop(0, HEADS - 1, step, 0)
                values(HEADS - 1, g, kb, (HEADS - 1) % 2)

        def finish(g):
            result = lax.dot_general(
                att[...], wout[...], (((0,), (0,)), ((), ())), preferred_element_type=F32
            )
            for k in range(4):
                d = own_chunk(g, k)
                here = pl.ds(k * cells, cells)
                obuf[g, here, :] = (result[k * cells : (k + 1) * cells] + raw[d].astype(F32)).astype(BF16)
            for k in (3, 2, 1, 0):
                if g == 0 and k == 0:
                    own = jnp.logical_and(j == 0, my_lat == 0)

                    @pl.when(own)
                    def _():
                        own_out_copy().start()

                    @pl.when(jnp.logical_not(own))
                    def _():
                        out_copy(g, k).start()
                else:
                    out_copy(g, k).start()

        arrive(0)
        run([(0, 0)])
        arrive(1)
        run([(1, 0), (1, 1)])
        finish(1)
        run([(0, 1)])
        finish(0)

    for d in range(n):
        @pl.when(sends_to(d))
        def _():
            for h in (0, 1):
                if d == 0:
                    @pl.when(j != h)
                    def _():
                        field_copy(d, h).wait_send()
                else:
                    field_copy(d, h).wait_send()

    @pl.when(main)
    def _():
        for d in range(n):
            forward(d).wait_send()
        for g in (0, 1):
            for k in range(4):
                if g == 0 and k == 0:
                    @pl.when(jnp.logical_not(jnp.logical_and(j == 0, my_lat == 0)))
                    def _():
                        out_copy(g, k).wait_send()
                else:
                    out_copy(g, k).wait_send()

    for r in range(rows):
        pltpu.make_async_copy(fields_ref.at[0], out_ref.at[r], out_recv.at[r]).wait()


def body(n, fields, norm_gain, w_qkv, w_out):
    rows, cells, width = fields.shape
    hw = width // HEADS
    span, keys = 4 * cells, 8 * cells
    hbm = pl.BlockSpec(memory_space=pl.ANY)
    scratch = [
        pltpu.VMEM((rows, cells, width), BF16),
        pltpu.VMEM((1, width), F32),
        pltpu.VMEM((width, 3 * width), BF16),
        pltpu.VMEM((width, width), BF16),
        pltpu.VMEM((n, cells, width), BF16),
        pltpu.VMEM((2, cells, width), BF16),
        pltpu.VMEM((n * cells, 2 * width), BF16),
        pltpu.VMEM((2 * width, n * cells), BF16),
        pltpu.VMEM((2, 2 * width, span), BF16),
        pltpu.VMEM((2 * width, span), BF16),
        pltpu.VMEM((2, keys, span), F32),
        pltpu.VMEM((2, HEADS, 1, span), F32),
        pltpu.VMEM((2, HEADS, 2 * hw, span), F32),
        pltpu.VMEM((2, 2, 1, span), F32),
        pltpu.VMEM((width, span), BF16),
        pltpu.VMEM((2, span, width), BF16),
        pltpu.SemaphoreType.DMA((4,)),
        pltpu.SemaphoreType.DMA((n, 2)),
        pltpu.SemaphoreType.DMA((n, 2)),
        pltpu.SemaphoreType.DMA((n,)),
        pltpu.SemaphoreType.DMA((2, 4)),
        pltpu.SemaphoreType.DMA((rows,)),
        pltpu.SemaphoreType.REGULAR((n // 2 - 1,)),
    ]
    return pl.pallas_call(
        functools.partial(kernel, n),
        out_shape=jax.ShapeDtypeStruct(fields.shape, fields.dtype),
        in_specs=[hbm] * 4,
        out_specs=hbm,
        scratch_shapes=scratch,
        compiler_params=pltpu.CompilerParams(collective_id=0, has_side_effects=True),
        name="axial",
    )(fields, norm_gain.reshape(1, width), w_qkv, w_out)


def solution(mesh):
    return jax.shard_map(
        functools.partial(body, mesh.shape["lon"]),
        mesh=mesh,
        in_specs=(P(("groups", "lat"), "lon", None), P(), P(), P()),
        out_specs=P(("groups", "lat"), "lon", None),
        check_vma=False,
    )
```

time: 116 us -> 68.2 us (0.59)
  Pallas kernels: 0 us -> 65.4 us
  waiting for transfers between devices: 30.6 us -> 0 us
  blocking collectives: 23.7 us -> 0 us
  matrix products: 21.1 us -> 0 us
  starting transfers between devices: 17 us -> 0 us
  other arithmetic: 11.7 us -> 0 us
  local copies, waits for them, and re-layouts: 10.9 us -> 1.62 us
    pallas_call x0 -> x1, Pallas kernels: none -> 65.4 us  [body(): pl.pallas_call(functools.partial(kernel, n), out_shape=jax.ShapeDtypeStru...]
    all_to_all x1 -> x0, waiting for transfers between devices: 30.6 us -> none  [body(): lax.all_to_all(stacked, 'lon', split_axis=0, concat_axis=2, tiled=True)]
    all_to_all x1 -> x0, blocking collectives: 23.7 us -> none  [body(): lax.all_to_all(results, 'lon', split_axis=2, concat_axis=0, tiled=True)]
    dot_general x26 -> x0, matrix products: 21.1 us -> none  [the longest x12 9.82 us: one_block(): jnp.dot(query_block, item_keys.T, preferred_element_type=jnp.float32)]
    all_to_all x1 -> x0, starting transfers between devices: 17 us -> none  [body(): lax.all_to_all(stacked, 'lon', split_axis=0, concat_axis=2, tiled=True)]
    reduce_sum x14 -> x0, other arithmetic: 10.8 us -> none  [the longest x12 8.51 us: one_block(): totals = jnp.sum(expd, axis=-1, keepdims=True)]
    unnamed x9 -> x1, local copies, waits for them, and re-layouts: 7.33 us -> 1.62 us
    while x4 -> x0, local copies, waits for them, and re-layouts: 1.52 us -> none  [the longest x1 1.35 us: attend_items(): results = lax.map(one_item, flat)]
  transfers between devices with their start and end apart: 1 -> 0, of which waited for: 1 -> 0; matrix products, arithmetic and copies ran while one was open for 0% -> 0% of each run, Pallas kernels for 0% -> 0%
where the time goes in v1:
time: 68.2 us; the launch traced here: 67 us
  Pallas kernels  65.4 us (96%)
  local copies, waits for them, and re-layouts  1.62 us (2%)
    pallas_call x1, Pallas kernels, body(): pl.pallas_call(functools.partial(kernel, n), out_shape=jax.ShapeDtypeStru...  65.4 us
    unnamed x1, local copies, waits for them, and re-layouts  1.62 us

profile of v1, /device:TPU:84, one launch (start us, length us, event | category | flops | bytes accessed | tf_op | source)
XLA Modules:
  0.0 67.0 jit_solution(5372722090035377357)
XLA Ops:
  0.0 65.4 %axial.1 = bf16[6,128,128]{2,1,0:T(8,128)(2,1)} custom-call(bf16[6,128,128]{2,1,0:T(8,128)(2,1)} %fields_ref.1, f32[1,128]{1,0:T(1,128)} %bitcast.1, bf16[128,384]{1,0:T(8,128)(2,1)} %wqkv_ref.1, bf16[128,128]{1,0:T(8,128)(2,1)} %wout_ref.1), custom_call_target="tpu_custom_call" | custom-call | tf_op jit(solution)/shard_map/axial/pallas_call | solution.py:339
  65.4 1.6 %copy.6 = bf16[6,128,128]{2,1,0:T(8,128)(2,1)} copy(bf16[6,128,128]{2,1,0:T(8,128)(2,1)} %axial.1) | data formatting | bytes 393216

commit v2 on v1

v2 whole, which is shorter than its diff:
```python
import functools
import math

import jax
import jax.numpy as jnp
from jax import lax
from jax.experimental import pallas as pl
from jax.experimental.pallas import tpu as pltpu
from jax.sharding import PartitionSpec as P

HEADS = 8
LOG2E = math.log2(math.e)
LOW = -1e30
AHEAD = 2
PLAN = [[], [(1, 0), (1, 1)], [(2, 0), (2, 1), (2, 2)], [(2, 3), (3, 0), (3, 1), (3, 2), (3, 3), (1, 2), (1, 3), (0, 0), (0, 1), (0, 2), (0, 3)]]
F32 = jnp.float32
BF16 = jnp.bfloat16
MESH = pl.DeviceIdType.MESH


def kernel(
    n,
    fields_ref, gain_ref, wqkv_ref, wout_ref, out_ref,
    xin, gain, wqkv, wout, raw, nbuf, kd, vt, qt, sbuf0, sbuf1, sbuf2, sbuf3, mst, ost, alpha, att, obuf,
    load_sem, raw_send, raw_recv, fwd_send, out_send, out_recv, ready,
):
    rows, cells, width = xin.shape
    total_rows = 2 * rows
    half = cells // 2
    hw = width // HEADS
    span = 2 * cells
    tile = 2 * cells
    keys = 4 * cells
    sbufs = (sbuf0, sbuf1, sbuf2, sbuf3)

    p = lax.axis_index("lon")
    j = lax.axis_index("lat")
    right = {"lon": lax.rem(p + 1, n), "lat": j}
    left = {"lon": lax.rem(p + n - 1, n), "lat": j}
    partner = {"lon": p, "lat": 1 - j}

    loads = [
        pltpu.make_async_copy(fields_ref, xin, load_sem.at[0]),
        pltpu.make_async_copy(gain_ref, gain, load_sem.at[1]),
        pltpu.make_async_copy(wqkv_ref, wqkv, load_sem.at[2]),
        pltpu.make_async_copy(wout_ref, wout, load_sem.at[3]),
    ]
    for load in loads:
        load.start()

    barrier = pltpu.get_barrier_semaphore()
    for dist in range(n // 4, 0, -1):
        for step in {dist, n - dist}:
            for core in (0, 1):
                pl.semaphore_signal(
                    barrier, inc=1, device_id={"lon": lax.rem(p + step, n), "lat": core}, device_id_type=MESH
                )
    pl.semaphore_signal(barrier, inc=1, device_id=partner, device_id_type=MESH)

    def row_of(x):
        return (x * total_rows + n - 1) // n

    def takes_row(x):
        return (row_of(x) * n) // total_rows == x

    my_row = row_of(p)
    main = takes_row(p)
    my_lat = my_row // rows
    my_r = lax.rem(my_row, rows)

    def field_copy(d, h):
        x = lax.rem(p + n - d, n)
        r = lax.rem(row_of(x), rows)
        return pltpu.make_async_remote_copy(
            src_ref=xin.at[r, pl.ds(h * half, half)],
            dst_ref=raw.at[d, pl.ds(h * half, half)],
            send_sem=raw_send.at[d, h],
            recv_sem=raw_recv.at[d, h],
            device_id={"lon": x, "lat": h},
            device_id_type=MESH,
        )

    def own_field_copy(h):
        return pltpu.make_async_copy(
            fields_ref.at[my_r, pl.ds(h * half, half)], raw.at[0, pl.ds(h * half, half)], raw_recv.at[0, h]
        )

    def sends_to(d):
        x = lax.rem(p + n - d, n)
        return jnp.logical_and(takes_row(x), row_of(x) // rows == j)

    def start_fields(d):
        @pl.when(sends_to(d))
        def _():
            for h in (0, 1):
                if d == 0:
                    @pl.when(j == h)
                    def _():
                        own_field_copy(h).start()

                    @pl.when(j != h)
                    def _():
                        field_copy(d, h).start()
                else:
                    field_copy(d, h).start()

    def forward(d):
        return pltpu.make_async_remote_copy(
            src_ref=raw.at[d, pl.ds(j * half, half)],
            dst_ref=raw.at[d, pl.ds(j * half, half)],
            send_sem=fwd_send.at[d],
            recv_sem=raw_recv.at[d, j],
            device_id=partner,
            device_id_type=MESH,
        )

    def wait_half(d, h):
        pltpu.make_async_copy(
            fields_ref.at[0, pl.ds(0, half)], raw.at[d, pl.ds(h * half, half)], raw_recv.at[d, h]
        ).wait()

    def take(d):
        wait_half(d, j)
        forward(d).start()

    loads[0].wait()
    pl.semaphore_wait(barrier, n + 1)
    for step in (n // 4, n - n // 4):
        pl.semaphore_signal(
            ready.at[0], inc=1, device_id={"lon": lax.rem(p + step, n), "lat": j}, device_id_type=MESH
        )
    start_fields(0)
    for dist in range(1, n // 4 + 1):
        start_fields(dist)
        start_fields(n - dist)
    pl.semaphore_wait(ready.at[0], 2)
    for dist in range(n // 2, n // 4, -1):
        start_fields(dist)
        if dist < n // 2:
            start_fields(n - dist)

    for load in loads[1:]:
        load.wait()

    def stage_chunks(g):
        return (2 * g, 2 * g + 1), (n - 1 - 2 * g, n - 2 - 2 * g)

    def own_chunk(g, k):
        return 2 * g + k + j * (n - 1 - 4 * g - 2 * k)

    def order_of(s):
        return s + s // 2 - 2 * (s // 3)

    def out_copy(s, k):
        d = own_chunk(order_of(s), k)
        return pltpu.make_async_remote_copy(
            src_ref=obuf.at[s, pl.ds(k * cells, cells)],
            dst_ref=out_ref.at[my_r],
            send_sem=out_send.at[s, k],
            recv_sem=out_recv.at[my_r],
            device_id={"lon": lax.rem(p + d, n), "lat": my_lat},
            device_id_type=MESH,
        )

    own_out = jnp.logical_and(j == 0, my_lat == 0)

    def own_out_copy():
        return pltpu.make_async_copy(obuf.at[0, pl.ds(0, cells)], out_ref.at[my_r], out_recv.at[my_r])

    @pl.when(main)
    def _():
        wq = wqkv[:, :width]
        wk = wqkv[:, width : 2 * width]
        wv = wqkv[:, 2 * width :]
        for h in range(HEADS):
            vt[pl.ds(2 * hw * h + hw, hw), :] = jnp.ones((hw, n * cells), BF16)

        def clear(h, carry):
            for s in range(4):
                mst[s, h] = jnp.full(mst.shape[2:], LOW, F32)
                ost[s, h] = jnp.zeros(ost.shape[2:], F32)
            return carry

        lax.fori_loop(0, HEADS, clear, 0)

        def project(slot, d, place):
            x = raw[d].astype(F32)
            center = jnp.mean(x, axis=-1, keepdims=True)
            y = x - center
            spread = jnp.mean(y * y, axis=-1, keepdims=True)
            normed = (y * lax.rsqrt(spread + 1e-05) * gain[...]).astype(BF16)
            nbuf[place] = normed
            where = pl.ds(slot * cells, cells)
            k = jnp.dot(normed, wk, preferred_element_type=F32).astype(BF16)
            kd[where, :width] = k
            kd[where, width:] = k
            v = lax.dot_general(wv, normed, (((0,), (1,)), ((), ())), preferred_element_type=F32).astype(BF16)
            for h in range(HEADS):
                vt[2 * hw * h : 2 * hw * h + hw, where] = v[hw * h : hw * h + hw]

        def arrive(s):
            sides = stage_chunks(order_of(s))
            for k in (0, 1):
                for side in sides:
                    take(side[k])
            for k in (0, 1):
                for place in (0, 1):
                    d = sides[place][k]
                    wait_half(d, 1 - j)
                    project(4 * s + 2 * place + k, d, place)
                q = lax.dot_general(wq, nbuf[j], (((0,), (1,)), ((), ())), preferred_element_type=F32)
                q = (q * (1.0 / math.sqrt(hw))).astype(BF16).astype(F32) * LOG2E
                high = q.astype(BF16)
                low = (q - high.astype(F32)).astype(BF16)
                where = pl.ds(k * cells, cells)
                qt[s, :width, where] = high
                qt[s, width:, where] = low

        def score_steps(unit, slot):
            heads, qb, kg = unit
            high = {}

            def queries(h):
                gap = jnp.zeros((hw, span), BF16)
                return jnp.concatenate(
                    [
                        qt[qb, pl.ds(base + hw * other, hw), :] if other == h else gap
                        for base in (0, width)
                        for other in range(HEADS)
                    ],
                    axis=0,
                )

            of = [queries(h) for h in heads]

            def step(t):
                for i, q in enumerate(of):
                    where = pl.ds(pl.multiple_of(kg * keys, keys) + t * tile, tile)
                    s = jnp.dot(kd[where, :], q, preferred_element_type=F32)
                    sbufs[slot][i, pl.ds(t * tile, tile), :] = s
                    peak = jnp.max(s.reshape(tile // 8, 8, span), axis=0)
                    high[i] = peak if t == 0 else jnp.maximum(high[i], peak)

            def end():
                for i, h in enumerate(heads):
                    old = mst[qb, h]
                    new = jnp.maximum(old, jnp.max(high[i], axis=0, keepdims=True))
                    mst[qb, h] = new
                    alpha[slot, i, 0] = new
                    alpha[slot, i, 1] = jnp.exp2(old - new)

            return step, end

        def value_steps(unit, slot):
            heads, qb, kg = unit
            total = {i: ost[qb, h] * alpha[slot, i, 1] for i, h in enumerate(heads)}

            def step(t):
                for i, h in enumerate(heads):
                    e = jnp.exp2(sbufs[slot][i, pl.ds(t * tile, tile), :] - alpha[slot, i, 0]).astype(BF16)
                    where = pl.ds(pl.multiple_of(kg * keys, keys) + t * tile, tile)
                    v = vt[pl.ds(2 * hw * h, 2 * hw), where]
                    total[i] = total[i] + jnp.dot(v, e, preferred_element_type=F32)

            def end():
                for i, h in enumerate(heads):
                    ost[qb, h] = total[i]
                    att[qb, pl.ds(h * hw, hw), :] = (total[i][:hw] / total[i][hw:]).astype(BF16)

            return step, end

        def both(score_of, value_of):
            a = None if score_of is None else score_steps(*score_of)
            b = None if value_of is None else value_steps(*value_of)
            for t in range(keys // tile):
                if a:
                    a[0](t)
                if b:
                    b[0](t)
            if a:
                a[1]()
            if b:
                b[1]()

        units = HEADS // 2

        def run(combo, count, final):
            def unit(i, a):
                qb, kg = combo(i + a // units)
                a = a % units
                return ((2 * a, 2 * a + 1), qb, kg), a

            for a in range(AHEAD):
                both(unit(0, a), None)

            def step(i, carry):
                for a in range(units):
                    both(unit(i, a + AHEAD), unit(i, a))
                if final:
                    qb, kg = combo(i)

                    @pl.when(kg == 3)
                    def _():
                        finish(qb)

                return carry

            if count > 1:
                lax.fori_loop(0, count - 1, step, 0)
            for a in range(units):
                both(unit(count - 1, a + AHEAD) if a + AHEAD < units else None, unit(count - 1, a))
            if final:
                finish(combo(count - 1)[0])

        def finish(s):
            result = lax.dot_general(
                att[s], wout[...], (((0,), (0,)), ((), ())), preferred_element_type=F32
            )
            group = order_of(s)
            for k in (1, 0):
                here = pl.ds(k * cells, cells)
                d = own_chunk(group, k)
                obuf[s, here, :] = (result[k * cells : (k + 1) * cells] + raw[d].astype(F32)).astype(BF16)
                if k == 0:
                    own = jnp.logical_and(own_out, s == 0)

                    @pl.when(own)
                    def _():
                        own_out_copy().start()

                    @pl.when(jnp.logical_not(own))
                    def _():
                        out_copy(s, k).start()
                else:
                    out_copy(s, k).start()

        def pick(values, i):
            count = len(values)
            got = values[0]
            for k in range(1, count):
                if values[k] != values[k - 1]:
                    got = got + (values[k] - values[k - 1]) * ((i + count - k) // count)
            return got

        for s, combos in enumerate(PLAN):
            arrive(s)
            if combos:
                blocks, groups = zip(*combos)
                run(lambda i, b=blocks, g=groups: (pick(b, i), pick(g, i)), len(combos), s == 3)

    for d in range(n):
        @pl.when(sends_to(d))
        def _():
            for h in (0, 1):
                if d == 0:
                    @pl.when(j != h)
                    def _():
                        field_copy(d, h).wait_send()
                else:
                    field_copy(d, h).wait_send()

    @pl.when(main)
    def _():
        for d in range(n):
            forward(d).wait_send()
        for s in range(4):
            for k in (0, 1):
                if s == 0 and k == 0:
                    @pl.when(jnp.logical_not(own_out))
                    def _():
                        out_copy(s, k).wait_send()
                else:
                    out_copy(s, k).wait_send()

    for r in range(rows):
        pltpu.make_async_copy(fields_ref.at[0], out_ref.at[r], out_recv.at[r]).wait()


def body(n, fields, norm_gain, w_qkv, w_out):
    rows, cells, width = fields.shape
    hw = width // HEADS
    span = 2 * cells
    hbm = pl.BlockSpec(memory_space=pl.ANY)
    scratch = [
        pltpu.VMEM((rows, cells, width), BF16),
        pltpu.VMEM((1, width), F32),
        pltpu.VMEM((width, 3 * width), BF16),
        pltpu.VMEM((width, width), BF16),
        pltpu.VMEM((n, cells, width), BF16),
        pltpu.VMEM((2, cells, width), BF16),
        pltpu.VMEM((n * cells, 2 * width), BF16),
        pltpu.VMEM((2 * width, n * cells), BF16),
        pltpu.VMEM((4, 2 * width, span), BF16),
        pltpu.VMEM((2, 4 * cells, span), F32),
        pltpu.VMEM((2, 4 * cells, span), F32),
        pltpu.VMEM((2, 4 * cells, span), F32),
        pltpu.VMEM((2, 4 * cells, span), F32),
        pltpu.VMEM((4, HEADS, 1, span), F32),
        pltpu.VMEM((4, HEADS, 2 * hw, span), F32),
        pltpu.VMEM((4, 2, 2, 1, span), F32),
        pltpu.VMEM((4, width, span), BF16),
        pltpu.VMEM((4, span, width), BF16),
        pltpu.SemaphoreType.DMA((4,)),
        pltpu.SemaphoreType.DMA((n, 2)),
        pltpu.SemaphoreType.DMA((n, 2)),
        pltpu.SemaphoreType.DMA((n,)),
        pltpu.SemaphoreType.DMA((4, 2)),
        pltpu.SemaphoreType.DMA((rows,)),
        pltpu.SemaphoreType.REGULAR((1,)),
    ]
    return pl.pallas_call(
        functools.partial(kernel, n),
        out_shape=jax.ShapeDtypeStruct(fields.shape, fields.dtype),
        in_specs=[hbm] * 4,
        out_specs=hbm,
        scratch_shapes=scratch,
        compiler_params=pltpu.CompilerParams(collective_id=0, has_side_effects=True),
        name="axial",
    )(fields, norm_gain.reshape(1, width), w_qkv, w_out)


def solution(mesh):
    return jax.shard_map(
        functools.partial(body, mesh.shape["lon"]),
        mesh=mesh,
        in_specs=(P(("groups", "lat"), "lon", None), P(), P(), P()),
        out_specs=P(("groups", "lat"), "lon", None),
        check_vma=False,
    )
```

time: 68.2 us -> 54.7 us (0.80)
  Pallas kernels: 65.4 us -> 52.3 us
    pallas_call x1, Pallas kernels: 65.4 us -> 52.3 us  [body(): pl.pallas_call(functools.partial(kernel, n), out_shape=jax.ShapeDtypeStru...]
where the time goes in v2:
time: 54.7 us; the launch traced here: 53.9 us
  Pallas kernels  52.3 us (96%)
  local copies, waits for them, and re-layouts  1.62 us (3%)
    pallas_call x1, Pallas kernels, body(): pl.pallas_call(functools.partial(kernel, n), out_shape=jax.ShapeDtypeStru...  52.3 us
    unnamed x1, local copies, waits for them, and re-layouts  1.62 us

profile of v2, /device:TPU:84, one launch (start us, length us, event | category | flops | bytes accessed | tf_op | source)
XLA Modules:
  0.0 53.9 jit_solution(10946177071726620960)
XLA Ops:
  0.0 52.3 %axial.1 = bf16[6,128,128]{2,1,0:T(8,128)(2,1)} custom-call(bf16[6,128,128]{2,1,0:T(8,128)(2,1)} %fields_ref.1, f32[1,128]{1,0:T(1,128)} %bitcast.1, bf16[128,384]{1,0:T(8,128)(2,1)} %wqkv_ref.1, bf16[128,128]{1,0:T(8,128)(2,1)} %wout_ref.1), custom_call_target="tpu_custom_call" | custom-call | tf_op jit(solution)/shard_map/axial/pallas_call | solution.py:411
  52.3 1.6 %copy.6 = bf16[6,128,128]{2,1,0:T(8,128)(2,1)} copy(bf16[6,128,128]{2,1,0:T(8,128)(2,1)} %axial.1) | data formatting | bytes 393216
